TPU v7x, 32 devices: a whole 2x2x4 slice. The times are simulated.
32 devices in a mesh: fsdp: 4 (over y, x), tp: 8 (over z, core).
Axes of the slice: x: 2, y: 2, z: 4, core: 2. Of those that a mesh axis runs over, the one named last changes fastest.
Arguments:
- tokens: bfloat16 [1024, 8192], P('fsdp', 'tp'), may hold values from -6 to 6
- out_grad: bfloat16 [1024, 8192], P('fsdp', 'tp'), may hold values from -6 to 6
- gate_weight: bfloat16 [8192, 1024], P('fsdp', 'tp'), may hold values from -0.0625 to 0.0625
- up_weight: bfloat16 [8192, 1024], P('fsdp', 'tp'), may hold values from -0.0625 to 0.0625
- down_weight: bfloat16 [1024, 8192], P('tp', 'fsdp'), may hold values from -0.1875 to 0.1875
Outputs:
- input_grad: bfloat16 [1024, 8192], P('fsdp', 'tp')
- gate_grad: float32 [8192, 1024], P('fsdp', 'tp')
- up_grad: float32 [8192, 1024], P('fsdp', 'tp')
- down_grad: float32 [1024, 8192], P('tp', 'fsdp')
All inputs are finite; a program needn't handle non-finite values.
Results may differ from a plain program's by a relative error of at most 0.0023.
Values may be sent and summed in bfloat16 or wider, within the bound.
A program may use at most 128 MiB of HBM per device.

v0:
```python
import math
import jax
import jax.numpy as jnp
from jax import lax
from jax.sharding import PartitionSpec as P


def over_all(shard, axis, dim, absorb, state):
    everything = jax.tree.map(lambda a: lax.all_gather(a, axis, axis=dim, tiled=True), shard)
    return absorb(state, everything, jnp.int32(0))


def own_rows(portion, rows, axis):
    count = rows * lax.axis_size(axis)
    return lax.psum_scatter(portion(jnp.int32(0), count), axis, scatter_dimension=0, tiled=True)


def column_term(left, right, start, count, factor):
    block = lax.dynamic_slice_in_dim(left, start, count, 1)
    product = lax.dot_general(
        block, right, (((0,), (0,)), ((), ())), preferred_element_type=jnp.float32
    )
    return product * factor


def body(tokens, out_grad, gate_weight, up_weight, down_weight):
    factor = 1.0 / math.sqrt(tokens.shape[0] * lax.axis_size("fsdp"))
    whole = lax.all_gather(tokens, "tp", axis=1, tiled=True)
    grads = lax.all_gather(out_grad, "tp", axis=1, tiled=True)
    gate_full, up_full = (
        lax.all_gather(gate_weight, "fsdp", axis=0, tiled=True),
        lax.all_gather(up_weight, "fsdp", axis=0, tiled=True),
    )
    gate = jnp.dot(whole, gate_full, preferred_element_type=jnp.float32)
    up = jnp.dot(whole, up_full, preferred_element_type=jnp.float32)

    def add_down(total, piece, start):
        columns = lax.dynamic_slice_in_dim(grads, start, piece.shape[1], 1)
        return total + lax.dot_general(
            columns, piece, (((1,), (1,)), ((), ())), preferred_element_type=jnp.float32
        )

    initial = jnp.zeros((whole.shape[0], down_weight.shape[0]), jnp.float32)
    hidden_grad = over_all(down_weight, "fsdp", 1, add_down, initial)
    squashed = jax.nn.sigmoid(gate)
    activated = gate * squashed
    slope = squashed * (1.0 + gate * (1.0 - squashed))
    hidden = (activated * up).astype(jnp.bfloat16)
    gate_delta = (hidden_grad * up * slope).astype(jnp.bfloat16)
    up_delta = (hidden_grad * activated).astype(jnp.bfloat16)
    partial_term = jnp.dot(gate_delta, gate_full.T, preferred_element_type=jnp.float32)
    partial_term = partial_term + jnp.dot(up_delta, up_full.T, preferred_element_type=jnp.float32)
    input_grad = lax.psum_scatter(partial_term, "tp", scatter_dimension=1, tiled=True).astype(
        jnp.bfloat16
    )
    rows_here = gate_weight.shape[0]

    def joint_term(start, count):
        return jnp.concatenate(
            [
                column_term(whole, gate_delta, start, count, factor),
                column_term(whole, up_delta, start, count, factor),
                column_term(grads, hidden, start, count, factor),
            ],
            axis=1,
        )

    summed = own_rows(joint_term, rows_here, "fsdp")
    width = gate_delta.shape[1]
    gate_grad = summed[:, :width]
    up_grad = summed[:, width : 2 * width]
    down_grad = summed[:, 2 * width :].T
    return (input_grad, gate_grad, up_grad, down_grad)


def solution(mesh):
    return jax.shard_map(
        body,
        mesh=mesh,
        in_specs=(
            P("fsdp", "tp"),
            P("fsdp", "tp"),
            P("fsdp", "tp"),
            P("fsdp", "tp"),
            P("tp", "fsdp"),
        ),
        out_specs=(P("fsdp", "tp"), P("fsdp", "tp"), P("fsdp", "tp"), P("tp", "fsdp")),
        check_vma=False,
    )
```

profile of v0, /device:TPU:0, one launch (start us, length us, event | category | flops | bytes accessed | tf_op | source)
XLA Modules:
  0.0 450.8 jit_solution(9459281939705098741)
XLA Ops:
  7.2 0.0 all-gather.14.cloned.1.call-start
  7.2 0.7 all-gather.14.cloned.1.call-update
  7.9 0.0 all-gather.10.cloned.1.call-start
  7.9 0.7 all-gather.10.cloned.1.call-update
  8.6 0.0 all-gather.12.cloned.1.call-start
  8.7 0.7 all-gather.12.cloned.1.call-update
  9.4 0.0 all-gather.8.cloned.1.call-start
  9.4 0.5 all-gather.8.cloned.1.call-update
  10.0 0.0 all-gather.6.cloned.1.call-start
  10.0 0.5 all-gather.6.cloned.1.call-update
  10.5 0.0 reduce-scatter.3.cloned.1.call-start
  10.6 37.2 %all-gather.14.cloned.1.call-done = bf16[8192,128]{1,0:T(8,128)(2,1)} async-done(((bf16[2048,128]{1,0:T(8,128)(2,1)}), bf16[8192,128]{1,0:T(8,128)(2,1)}) %all-gather.14.cloned.1.call-update) | async-done | bytes 2097168 | tf_op jit(solution)/shard_map/all_gather | solution.py:31
  47.8 48.5 %all-gather.10.cloned.1.call-done = bf16[256,8192]{1,0:T(8,128)(2,1)} async-done(((bf16[256,1024]{1,0:T(8,128)(2,1)}), bf16[256,8192]{1,0:T(8,128)(2,1)}) %all-gather.10.cloned.1.call-update) | async-done | bytes 4194320 | tf_op jit(solution)/shard_map/all_gather | solution.py:28
  96.3 4.1 fusion.7
  100.4 31.8 %all-gather.12.cloned.1.call-done = bf16[8192,128]{1,0:T(8,128)(2,1)} async-done(((bf16[2048,128]{1,0:T(8,128)(2,1)}), bf16[8192,128]{1,0:T(8,128)(2,1)}) %all-gather.12.cloned.1.call-update) | async-done | bytes 2097168 | tf_op jit(solution)/shard_map/all_gather | solution.py:32
  132.1 4.1 fusion.6
  136.2 0.0 copy-start.1
  136.2 32.8 %all-gather.8.cloned.1.call-done = bf16[128,8192]{1,0:T(8,128)(2,1)} async-done(((bf16[128,2048]{1,0:T(8,128)(2,1)}), bf16[128,8192]{1,0:T(8,128)(2,1)}) %all-gather.8.cloned.1.call-update) | async-done | bytes 2097168 | tf_op jit(solution)/shard_map/all_gather | solution.py:9
  169.0 48.4 %all-gather.6.cloned.1.call-done = bf16[256,8192]{1,0:T(8,128)(2,1)} async-done(((bf16[256,1024]{1,0:T(8,128)(2,1)}), bf16[256,8192]{1,0:T(8,128)(2,1)}) %all-gather.6.cloned.1.call-update) | async-done | bytes 4194320 | tf_op jit(solution)/shard_map/all_gather | solution.py:29
  217.4 4.1 multiply_convert_fusion.1
  221.5 0.0 copy-done.1
  221.5 0.0 copy-start.2
  221.5 1.3 fusion.8
  222.8 0.3 copy-done.2
  223.1 4.5 convolution_add_fusion
  227.6 0.0 reduce-scatter.3.cloned.1.call-update
  227.6 0.0 reduce-scatter.5.cloned.1.call-start
  227.6 0.0 copy-start
  227.6 3.1 fusion.1
  230.8 0.3 copy-done
  231.1 0.0 copy-start.3
  231.1 0.8 fusion.2
  231.9 2.1 copy-done.3
  234.0 0.8 fusion
  234.8 5.0 %pad_maximum_fusion = f32[8192,384]{0,1:T(8,128)} fusion(f32[8192,128]{0,1:T(8,128)S(1)} %fusion, f32[8192,128]{0,1:T(8,128)S(1)} %fusion.1, f32[8192,128]{0,1:T(8,128)S(1)} %fusion.2), kind=kLoop, calls=%fused_computation | loop fusion | flops 6291456 | bytes 25165824 | tf_op jit(solution)/shard_map/concatenate | solution.py:59
  239.8 0.0 reduce-scatter.5.cloned.1.call-update
  239.9 76.2 %reduce-scatter.3.cloned.1.call-done = f32[256,1024]{1,0:T(8,128)} async-done(((f32[256,8192]{1,0:T(8,128)}), f32[256,1024]{1,0:T(8,128)}) %reduce-scatter.3.cloned.1.call-update) | async-done | bytes 1048592 | tf_op jit(solution)/shard_map/reduce_scatter | solution.py:53
  316.1 2.1 convert_element_type.14
  318.2 120.1 %reduce-scatter.5.cloned.1.call-done = f32[2048,384]{0,1:T(8,128)} async-done(((f32[8192,384]{0,1:T(8,128)}), f32[2048,384]{0,1:T(8,128)}) %reduce-scatter.5.cloned.1.call-update) | async-done | bytes 3145744 | tf_op jit(solution)/shard_map/reduce_scatter | solution.py:15
  438.3 3.1 slice_bitcast_fusion
  441.4 1.3 copy.9
  442.7 1.3 copy.10
Async XLA Ops:
  7.2 40.6 %all-gather.14.cloned.1.call-start = ((), (), s32[]{:S(2)}) async-start(), calls=%async_computation.6 | async-start | bytes 2621440 | tf_op jit(solution)/shard_map/all_gather | solution.py:31
  7.9 88.4 %all-gather.10.cloned.1.call-start = ((), (), s32[]{:S(2)}) async-start(), calls=%async_computation.4 | async-start | bytes 4718592 | tf_op jit(solution)/shard_map/all_gather | solution.py:28
  8.6 123.5 %all-gather.12.cloned.1.call-start = ((), (), s32[]{:S(2)}) async-start(), calls=%async_computation.5 | async-start | bytes 2621440 | tf_op jit(solution)/shard_map/all_gather | solution.py:32
  9.4 159.6 %all-gather.8.cloned.1.call-start = ((), (), s32[]{:S(2)}) async-start(), calls=%async_computation.3 | async-start | bytes 2621440 | tf_op jit(solution)/shard_map/all_gather | solution.py:9
  10.0 207.4 %all-gather.6.cloned.1.call-start = ((), (), s32[]{:S(2)}) async-start(), calls=%async_computation.2 | async-start | bytes 4718592 | tf_op jit(solution)/shard_map/all_gather | solution.py:29
  10.5 305.5 %reduce-scatter.3.cloned.1.call-start = ((), (), s32[]{:S(2)}) async-start(), calls=%async_computation.7 | async-start | bytes 9437184 | tf_op jit(solution)/shard_map/reduce_scatter | solution.py:53
  136.2 85.3 %copy-start.1 = (bf16[8192,128]{1,0:T(8,128)(2,1)S(1)}, bf16[8192,128]{1,0:T(8,128)(2,1)}, u32[]{:S(2)}) copy-start(bf16[8192,128]{1,0:T(8,128)(2,1)} %all-gather.14.cloned.1.call-done) | copy-start | bytes 6291460
  221.5 1.6 copy-start.2
  227.6 210.7 %reduce-scatter.5.cloned.1.call-start = ((), (), s32[]{:S(2)}) async-start(), calls=%async_computation.8 | async-start | bytes 15728640 | tf_op jit(solution)/shard_map/reduce_scatter | solution.py:15
  227.6 3.5 copy-start
  231.1 2.9 copy-start.3
Sparse Core Ops, SparseCore 0:
  9.8 37.8 all-gather.13
  49.4 46.8 all-gather.9
  98.1 33.9 all-gather.11
  133.8 35.1 all-gather.7
  170.5 46.8 all-gather.5
  227.7 88.3 reduce-scatter.2
  319.2 119.0 reduce-scatter.4
where the time goes:
time: 451 us
  waiting for transfers between devices  398 us (88%)
  matrix products  22.8 us (5%)
  between operations  14.2 us (3%)
  local copies, waits for them, and re-layouts  8.46 us (2%)
  other arithmetic  7.1 us (2%)
    reduce_scatter x1, waiting for transfers between devices, own_rows(): lax.psum_scatter(portion(jnp.int32(0), count), axis, scatter_dimension=0,...  120 us
    reduce_scatter x1, waiting for transfers between devices, body(): lax.psum_scatter(partial_term, 'tp', scatter_dimension=1, tiled=True)  76.2 us
    all_gather x1, waiting for transfers between devices, body(): whole = lax.all_gather(tokens, 'tp', axis=1, tiled=True)  48.5 us
    all_gather x1, waiting for transfers between devices, body(): grads = lax.all_gather(out_grad, 'tp', axis=1, tiled=True)  48.4 us
    all_gather x1, waiting for transfers between devices, body(): lax.all_gather(gate_weight, 'fsdp', axis=0, tiled=True)  37.2 us
    all_gather x1, waiting for transfers between devices, over_all(): lax.all_gather(a, axis, axis=dim, tiled=True)  32.8 us
    all_gather x1, waiting for transfers between devices, body(): lax.all_gather(up_weight, 'fsdp', axis=0, tiled=True)  31.8 us
  transfers between devices with their start and end apart: 7, of which 7 were waited for; matrix products, arithmetic and copies ran while one was open for 4% of the time, Pallas kernels for 0%

commit v1 on v0

--- a/solution.py
+++ b/solution.py
@@ -25,8 +25,11 @@
 
 def body(tokens, out_grad, gate_weight, up_weight, down_weight):
     factor = 1.0 / math.sqrt(tokens.shape[0] * lax.axis_size("fsdp"))
-    whole = lax.all_gather(tokens, "tp", axis=1, tiled=True)
-    grads = lax.all_gather(out_grad, "tp", axis=1, tiled=True)
+    whole, grads = jnp.split(
+        lax.all_gather(jnp.concatenate([tokens, out_grad], axis=0), "tp", axis=1, tiled=True),
+        [tokens.shape[0]],
+        0,
+    )
     gate_full, up_full = (
         lax.all_gather(gate_weight, "fsdp", axis=0, tiled=True),
         lax.all_gather(up_weight, "fsdp", axis=0, tiled=True),

time: 451 us -> 439 us (0.973)
  waiting for transfers between devices: 398 us -> 383 us
    all_gather x2 -> x1, waiting for transfers between devices: 96.9 us -> 84.2 us  [body(): lax.all_gather(jnp.concatenate([tokens, out_grad], axis=0), 'tp', axis=1,...]
  transfers between devices with their start and end apart: 7 -> 6, of which waited for: 7 -> 6; matrix products, arithmetic and copies ran while one was open for 4% -> 6% of each run, Pallas kernels for 0% -> 0%
where the time goes in v1:
time: 439 us
  waiting for transfers between devices  383 us (87%)
  matrix products  25.2 us (6%)
  between operations  14.2 us (3%)
  other arithmetic  9.29 us (2%)
  local copies, waits for them, and re-layouts  6.94 us (2%)
    reduce_scatter x1, waiting for transfers between devices, own_rows(): lax.psum_scatter(portion(jnp.int32(0), count), axis, scatter_dimension=0,...  120 us
    all_gather x1, waiting for transfers between devices, body(): lax.all_gather(jnp.concatenate([tokens, out_grad], axis=0), 'tp', axis=1,...  84.2 us
    reduce_scatter x1, waiting for transfers between devices, body(): lax.psum_scatter(partial_term, 'tp', scatter_dimension=1, tiled=True)  76.5 us
    all_gather x1, waiting for transfers between devices, body(): lax.all_gather(gate_weight, 'fsdp', axis=0, tiled=True)  36.2 us
    all_gather x1, waiting for transfers between devices, over_all(): lax.all_gather(a, axis, axis=dim, tiled=True)  32.8 us
    all_gather x1, waiting for transfers between devices, body(): lax.all_gather(up_weight, 'fsdp', axis=0, tiled=True)  31.4 us
  transfers between devices with their start and end apart: 6, of which 6 were waited for; matrix products, arithmetic and copies ran while one was open for 6% of the time, Pallas kernels for 0%

profile of v1, /device:TPU:0, one launch (start us, length us, event | category | flops | bytes accessed | tf_op | source)
XLA Modules:
  0.0 439.0 jit_solution(5686850107040670691)
XLA Ops:
  7.2 0.0 all-gather.11.cloned.1.call-start
  7.2 0.7 all-gather.11.cloned.1.call-update
  7.9 0.0 all-gather.5.cloned.1.call-start
  7.9 2.2 pad_maximum_fusion.1
  10.2 0.0 all-gather.5.cloned.1.call-update
  10.2 0.0 all-gather.9.cloned.1.call-start
  10.3 0.7 all-gather.9.cloned.1.call-update
  10.9 0.0 all-gather.7.cloned.1.call-start
  11.0 0.5 all-gather.7.cloned.1.call-update
  11.5 0.0 reduce-scatter.3.cloned.1.call-start
  11.6 36.2 %all-gather.11.cloned.1.call-done = bf16[8192,128]{1,0:T(8,128)(2,1)} async-done(((bf16[2048,128]{1,0:T(8,128)(2,1)}), bf16[8192,128]{1,0:T(8,128)(2,1)}) %all-gather.11.cloned.1.call-update) | async-done | bytes 2097168 | tf_op jit(solution)/shard_map/all_gather | solution.py:34
  47.8 84.2 %all-gather.5.cloned.1.call-done = bf16[512,8192]{1,0:T(8,128)(2,1)} async-done(((bf16[512,1024]{1,0:T(8,128)(2,1)}), bf16[512,8192]{1,0:T(8,128)(2,1)}) %all-gather.5.cloned.1.call-update) | async-done | bytes 8388624 | tf_op jit(solution)/shard_map/all_gather | solution.py:29
  132.0 4.1 fusion.5
  136.1 31.4 %all-gather.9.cloned.1.call-done = bf16[8192,128]{1,0:T(8,128)(2,1)} async-done(((bf16[2048,128]{1,0:T(8,128)(2,1)}), bf16[8192,128]{1,0:T(8,128)(2,1)}) %all-gather.9.cloned.1.call-update) | async-done | bytes 2097168 | tf_op jit(solution)/shard_map/all_gather | solution.py:35
  167.5 4.1 fusion.7
  171.7 0.0 copy-start
  171.7 32.8 %all-gather.7.cloned.1.call-done = bf16[128,8192]{1,0:T(8,128)(2,1)} async-done(((bf16[128,2048]{1,0:T(8,128)(2,1)}), bf16[128,8192]{1,0:T(8,128)(2,1)}) %all-gather.7.cloned.1.call-update) | async-done | bytes 2097168 | tf_op jit(solution)/shard_map/all_gather | solution.py:9
  204.5 4.1 multiply_convert_fusion.1
  208.6 0.0 copy-done
  208.6 0.0 copy-start.1
  208.6 1.3 fusion.12
  209.9 0.3 copy-done.1
  210.2 4.5 %convolution_add_fusion = f32[256,8192]{1,0:T(8,128)} fusion(f32[256,8192]{1,0:T(8,128)S(1)} %fusion.12, bf16[256,128]{1,0:T(8,128)(2,1)S(1)} %get-tuple-element.11, bf16[8192,128]{1,0:T(8,128)(2,1)S(1)} %copy-done.1), kind=kOutput, calls=%fused_computation.1 | convolution fusion | flops 538968064 | bytes 18939904 | tf_op jit(solution)/shard_map/dot_general | solution.py:55
  214.6 0.0 reduce-scatter.3.cloned.1.call-update
  214.7 0.0 reduce-scatter.5.cloned.1.call-start
  214.7 0.0 slice-start
  214.7 3.2 convolution_multiply_fusion.1
  217.9 0.0 slice-start.1
  217.9 3.2 convolution_multiply_fusion.2
  221.1 0.0 slice-done
  221.1 0.9 slice-done.1
  222.0 0.8 convolution_multiply_fusion
  222.8 5.0 %pad_maximum_fusion = f32[8192,384]{0,1:T(8,128)} fusion(f32[8192,128]{0,1:T(8,128)S(1)} %convolution_multiply_fusion, f32[8192,128]{0,1:T(8,128)S(1)} %convolution_multiply_fusion.1, f32[8192,128]{0,1:T(8,128)S(1)} %convolution_multiply_fusion.2), kind=kLoop, calls=%fused_computation | loop fusion | flops 6291456 | bytes 25165824 | tf_op jit(solution)/shard_map/concatenate | solution.py:62
  227.8 0.0 reduce-scatter.5.cloned.1.call-update
  227.8 76.5 %reduce-scatter.3.cloned.1.call-done = f32[256,1024]{1,0:T(8,128)} async-done(((f32[256,8192]{1,0:T(8,128)}), f32[256,1024]{1,0:T(8,128)}) %reduce-scatter.3.cloned.1.call-update) | async-done | bytes 1048592 | tf_op jit(solution)/shard_map/reduce_scatter | solution.py:56
  304.3 2.1 convert_element_type.14
  306.4 120.0 %reduce-scatter.5.cloned.1.call-done = f32[2048,384]{0,1:T(8,128)} async-done(((f32[8192,384]{0,1:T(8,128)}), f32[2048,384]{0,1:T(8,128)}) %reduce-scatter.5.cloned.1.call-update) | async-done | bytes 3145744 | tf_op jit(solution)/shard_map/reduce_scatter | solution.py:15
  426.4 3.1 slice_bitcast_fusion
  429.5 1.3 copy.9
  430.8 1.3 copy.10
  (1 shorter events, 0.0 us)
Async XLA Ops:
  7.2 40.6 %all-gather.11.cloned.1.call-start = ((), (), s32[]{:S(2)}) async-start(), calls=%async_computation.5 | async-start | bytes 2621440 | tf_op jit(solution)/shard_map/all_gather | solution.py:34
  7.9 124.1 %all-gather.5.cloned.1.call-start = ((), (), s32[]{:S(2)}) async-start(), calls=%async_computation.2 | async-start | bytes 9437184 | tf_op jit(solution)/shard_map/all_gather | solution.py:29
  10.2 157.3 %all-gather.9.cloned.1.call-start = ((), (), s32[]{:S(2)}) async-start(), calls=%async_computation.4 | async-start | bytes 2621440 | tf_op jit(solution)/shard_map/all_gather | solution.py:35
  10.9 193.5 %all-gather.7.cloned.1.call-start = ((), (), s32[]{:S(2)}) async-start(), calls=%async_computation.3 | async-start | bytes 2621440 | tf_op jit(solution)/shard_map/all_gather | solution.py:9
  11.5 292.8 %reduce-scatter.3.cloned.1.call-start = ((), (), s32[]{:S(2)}) async-start(), calls=%async_computation.6 | async-start | bytes 9437184 | tf_op jit(solution)/shard_map/reduce_scatter | solution.py:56
  171.7 36.9 %copy-start = (bf16[8192,128]{1,0:T(8,128)(2,1)S(1)}, bf16[8192,128]{1,0:T(8,128)(2,1)}, u32[]{:S(2)}) copy-start(bf16[8192,128]{1,0:T(8,128)(2,1)} %all-gather.11.cloned.1.call-done) | copy-start | bytes 6291460
  208.6 1.6 copy-start.1
  214.7 211.8 %reduce-scatter.5.cloned.1.call-start = ((), (), s32[]{:S(2)}) async-start(), calls=%async_computation.7 | async-start | bytes 15728640 | tf_op jit(solution)/shard_map/reduce_scatter | solution.py:15
  214.7 6.3 %slice-start = ((s8[8388608]{0:T(1024)(128)(4,1)}), s8[4194304]{0:T(1024)(128)(4,1)S(1)}, s32[]{:S(2)}) async-start(s8[8388608]{0:T(1024)(128)(4,1)} %bitcast.11), calls=%async_computation.8 | async-start | bytes 8388608
  217.9 4.1 slice-start.1
Sparse Core Ops, SparseCore 0:
  9.8 37.8 all-gather.10
  49.9 82.0 all-gather.4
  133.8 33.6 all-gather.8
  169.2 35.1 all-gather.6
  214.8 89.4 reduce-scatter.2
  307.3 119.0 reduce-scatter.4
